TPU v7x, 32 devices: a whole 2x2x4 slice. The times are simulated.
32 devices in a mesh: occ: 8 (over y, x, core), frag: 4 (over z).
Axes of the slice: x: 2, y: 2, z: 4, core: 2. Of those that a mesh axis runs over, the one named last changes fastest.
Arguments:
- factors: bfloat16 [32, 512, 1280], P(('frag', 'occ')), parts along dimension 0, may hold values from -1 to 1
- occ_energy: float32 [32], P('frag'), parts along dimension 0, may hold values from -2 to -0.3
- vir_energy: float32 [2048], P('frag'), parts along dimension 0, may hold values from 0.2 to 4
- coeffs: bfloat16 [4096, 512], P('frag'), parts along dimension 0, may hold values from -0.25 to 0.25
Outputs:
- back: bfloat16 [1280, 32, 1024], P('occ', 'frag'), parts along dimension 1
There are 4 independent parts, one for each index of `frag`. A program takes and returns all parts, laid end to end along the dimension named above; each array names one. Nothing has to cross between parts.
All inputs are finite; a program needn't handle non-finite values.
Results may differ from a plain program's by a relative error of at most 0.008.
Values may be sent and summed in bfloat16 or wider, within the bound.
A program may use at most 64 MiB of HBM per device.

v0:
```python
import jax
import jax.numpy as jnp
from jax import lax
from jax.sharding import PartitionSpec as P

OFFSETS = 3


def passed_along(block, axis, distance):
    devices = range(lax.axis_size(axis))
    route = [((i - distance) % len(devices), i) for i in devices]
    return lax.ppermute(block, axis, route)


def on_device(factors, occ_energy, vir_energy, coeffs):
    mine = factors[0]
    count = lax.axis_size("occ")
    index = lax.axis_index("occ")
    partners = []
    current = mine
    for offset in range(1, OFFSETS + 1):
        current = passed_along(current, "occ", -1)
        partners.append(current)
    own_energy = lax.dynamic_index_in_dim(occ_energy, index, 0, False)
    own = jnp.zeros((mine.shape[1], mine.shape[0]), jnp.float32)
    outgoing = []
    for offset in range(1, OFFSETS + 1):
        partner = partners[offset - 1]
        other_energy = lax.dynamic_index_in_dim(occ_energy, (index + offset) % count, 0, False)
        kmat = lax.dot_general(
            mine, partner, (((1,), (1,)), ((), ())), preferred_element_type=jnp.float32
        )
        denom = own_energy + other_energy - vir_energy[:, None] - vir_energy[None, :]
        amps = (kmat / denom).astype(jnp.bfloat16)
        own = own + lax.dot_general(
            partner, amps, (((0,), (1,)), ((), ())), preferred_element_type=jnp.float32
        )
        sent = lax.dot_general(
            mine, amps, (((0,), (0,)), ((), ())), preferred_element_type=jnp.float32
        )
        outgoing.append(sent.astype(jnp.bfloat16))
    incoming = jnp.zeros_like(own)
    for offset in range(1, OFFSETS + 1):
        arrived = passed_along(outgoing[offset - 1], "occ", offset)
        incoming = incoming + arrived.astype(jnp.float32)
    gamma = (own + incoming).astype(jnp.bfloat16)[None]
    slabs = lax.all_to_all(gamma, "occ", split_axis=1, concat_axis=0, tiled=True)
    return jnp.einsum("ipa,ma->pim", slabs, coeffs, preferred_element_type=jnp.float32).astype(
        jnp.bfloat16
    )


def solution(mesh):
    return jax.shard_map(
        on_device,
        mesh=mesh,
        in_specs=(P(("frag", "occ"), None, None), P("frag"), P("frag"), P("frag", None)),
        out_specs=P("occ", "frag", None),
        check_vma=False,
    )
```

profile of v0, /device:TPU:0, one launch (start us, length us, event | category | flops | bytes accessed | tf_op | source)
XLA Modules:
  0.0 173.1 jit_solution(9468343890820798394)
XLA Ops:
  0.0 3.4 %collective-permute-start = (bf16[512,1280]{1,0:T(8,128)(2,1)}, bf16[512,1280]{1,0:T(8,128)(2,1)}, u32[]{:S(2)}, u32[]{:S(2)}) collective-permute-start(bf16[512,1280]{1,0:T(8,128)(2,1)} %bitcast.56), channel_id=1, source_target_pairs={{4,0},{8,4},{12,8},{16,12},{20,16},{24,20},{28,24},{0,28},{5,1},{9... | collective-permute-start | bytes 3932168 | tf_op jit(solution)/shard_map/ppermute | solution.py:12
  3.4 15.4 %collective-permute-done = bf16[512,1280]{1,0:T(8,128)(2,1)} collective-permute-done((bf16[512,1280]{1,0:T(8,128)(2,1)}, bf16[512,1280]{1,0:T(8,128)(2,1)}, u32[]{:S(2)}, u32[]{:S(2)}) %collective-permute-start) | collective-permute-done | bytes 1310752 | tf_op jit(solution)/shard_map/ppermute | solution.py:12
  18.8 2.8 %collective-permute-start.1 = (bf16[512,1280]{1,0:T(8,128)(2,1)}, bf16[512,1280]{1,0:T(8,128)(2,1)S(1)}, u32[]{:S(2)}, u32[]{:S(2)}) collective-permute-start(bf16[512,1280]{1,0:T(8,128)(2,1)} %collective-permute-done), channel_id=1, source_target_pairs={{4,0},{8,4},{12,8},{16,12},{20,16},{24,20},{28,24},{0,28},{5,1},{9... | collective-permute-start | bytes 3932168 | tf_op jit(solution)/shard_map/ppermute | solution.py:12
  21.6 1.5 fusion.17
  27.5 9.5 %collective-permute-done.1 = bf16[512,1280]{1,0:T(8,128)(2,1)S(1)} collective-permute-done((bf16[512,1280]{1,0:T(8,128)(2,1)}, bf16[512,1280]{1,0:T(8,128)(2,1)S(1)}, u32[]{:S(2)}, u32[]{:S(2)}) %collective-permute-start.1) | collective-permute-done | bytes 1310752 | tf_op jit(solution)/shard_map/ppermute | solution.py:12
  37.1 2.7 %collective-permute-start.2 = (bf16[512,1280]{1,0:T(8,128)(2,1)S(1)}, bf16[512,1280]{1,0:T(8,128)(2,1)S(1)}, u32[]{:S(2)}, u32[]{:S(2)}) collective-permute-start(bf16[512,1280]{1,0:T(8,128)(2,1)S(1)} %collective-permute-done.1), channel_id=1, source_target_pairs={{4,0},{8,4},{12,8},{16,12},{20,16},{24,20},{28,24},{0,28},{5,1},{9... | collective-permute-start | bytes 3932168 | tf_op jit(solution)/shard_map/ppermute | solution.py:12
  39.8 2.7 %fusion.7 = bf16[512,512]{1,0:T(8,128)(2,1)S(1)} fusion(bf16[512,1280]{1,0:T(8,128)(2,1)} %collective-permute-done, f32[512]{0:T(512)} %param.6, f32[512]{0:T(512)S(1)} %get-tuple-element.6, bf16[1,512,1280]{2,1,0:T(8,128)(2,1)} %param.4), kind=kOutput, calls=%fused_computation.16 | convolution fusion | flops 671875072 | bytes 3149824 | tf_op jit(solution)/shard_map/dot_general | solution.py:30
  43.4 0.9 fusion.8
  45.3 22.8 %collective-permute-done.2 = bf16[512,1280]{1,0:T(8,128)(2,1)S(1)} collective-permute-done((bf16[512,1280]{1,0:T(8,128)(2,1)S(1)}, bf16[512,1280]{1,0:T(8,128)(2,1)S(1)}, u32[]{:S(2)}, u32[]{:S(2)}) %collective-permute-start.2) | collective-permute-done | bytes 1310752 | tf_op jit(solution)/shard_map/ppermute | solution.py:12
  68.0 0.9 fusion.9
  69.8 0.9 collective-permute-start.5
  70.7 2.2 %fusion.18 = f32[512,1280]{1,0:T(8,128)S(1)} fusion(bf16[512,512]{1,0:T(8,128)(2,1)S(1)} %fusion.7, bf16[512,1280]{1,0:T(8,128)(2,1)} %collective-permute-done), kind=kOutput, calls=%fused_computation.30 | convolution fusion | flops 671088640 | bytes 4456448 | tf_op jit(solution)/shard_map/dot_general | solution.py:35
  73.7 1.8 %collective-permute-done.3 = bf16[1280,512]{0,1:T(8,128)(2,1)S(1)} collective-permute-done((bf16[1280,512]{0,1:T(8,128)(2,1)S(1)}, bf16[1280,512]{0,1:T(8,128)(2,1)S(1)}, u32[]{:S(2)}, u32[]{:S(2)}) %collective-permute-start.3) | collective-permute-done | bytes 1310752 | tf_op jit(solution)/shard_map/ppermute | solution.py:12
  75.5 20.6 %collective-permute-done.4 = bf16[1280,512]{0,1:T(8,128)(2,1)S(1)} collective-permute-done((bf16[1280,512]{0,1:T(8,128)(2,1)S(1)}, bf16[1280,512]{0,1:T(8,128)(2,1)S(1)}, u32[]{:S(2)}, u32[]{:S(2)}) %collective-permute-start.4) | collective-permute-done | bytes 1310752 | tf_op jit(solution)/shard_map/ppermute | solution.py:12
  96.1 28.2 %collective-permute-done.5 = bf16[1280,512]{0,1:T(8,128)(2,1)S(1)} collective-permute-done((bf16[1280,512]{0,1:T(8,128)(2,1)S(1)}, bf16[1280,512]{0,1:T(8,128)(2,1)S(1)}, u32[]{:S(2)}, u32[]{:S(2)}) %collective-permute-start.5) | collective-permute-done | bytes 1310752 | tf_op jit(solution)/shard_map/ppermute | solution.py:12
  124.3 0.9 fusion.6
  125.3 4.1 %copy.9 = bf16[1,1280,512]{2,0,1:T(2,128)(2,1)} copy(bf16[1,1280,512]{1,2,0:T(8,128)(2,1)S(1)} %fusion.6) | data formatting | bytes 2621440 | tf_op jit(solution)/shard_map/broadcast_in_dim | solution.py:46
  129.9 9.5 %reduce = bf16[1280,512]{1,0:T(8,128)(2,1)S(1)} reduce(bf16[1280,1,512]{2,1,0:T(2,128)(2,1)} %bitcast.53, bf16[]{:T(256)} %broadcast.10), dimensions={1}, to_apply=%bitcast.38.reduce_sub_computation | reduce | bytes 2621442
  139.4 1.8 %reshape.14 = bf16[8,2,40960]{2,1,0:T(2,128)(2,1)} reshape(bf16[1280,512]{1,0:T(8,128)(2,1)S(1)} %reduce) | data formatting | bytes 2621440
  141.2 21.6 %all_to_all.12 = bf16[8,2,40960]{2,1,0:T(2,128)(2,1)S(1)} all-to-all(bf16[8,2,40960]{2,1,0:T(2,128)(2,1)} %reshape.14), channel_id=1, replica_groups=mesh['occ'=8,'frag'=4] {'occ'}, dimensions={0} | all-to-all | bytes 2621440 | tf_op jit(solution)/shard_map/all_to_all | solution.py:47
  162.8 3.6 %reshape.15 = bf16[1280,1,512]{2,1,0:T(2,128)(2,1)} reshape(bf16[8,2,40960]{2,1,0:T(2,128)(2,1)S(1)} %all_to_all.12) | data formatting | bytes 2621440
  166.5 2.1 %copy.11 = bf16[1,1280,512]{2,1,0:T(8,128)(2,1)S(1)} copy(bf16[1,1280,512]{2,0,1:T(2,128)(2,1)} %bitcast.54) | data formatting | bytes 2621440
  168.6 1.6 convert_bitcast_fusion
  170.2 2.9 %copy.10 = bf16[160,8,1024]{2,1,0:T(8,128)(2,1)} copy(bf16[160,8,1024]{2,0,1:T(8,128)(2,1)S(1)} %convert_bitcast_fusion) | data formatting | bytes 5242880 | tf_op jit(solution)/shard_map/convert_element_type | solution.py:48
  (14 shorter events, 4.9 us)
Async XLA Ops:
  0.0 168.6 %copy-start = (bf16[1024,512]{1,0:T(8,128)(2,1)S(1)}, bf16[1024,512]{1,0:T(8,128)(2,1)}, u32[]{:S(2)}) copy-start(bf16[1024,512]{1,0:T(8,128)(2,1)} %param.7) | copy-start | bytes 3145732
  0.0 18.8 %collective-permute-start = (bf16[512,1280]{1,0:T(8,128)(2,1)}, bf16[512,1280]{1,0:T(8,128)(2,1)}, u32[]{:S(2)}, u32[]{:S(2)}) collective-permute-start(bf16[512,1280]{1,0:T(8,128)(2,1)} %bitcast.56), channel_id=1, source_target_pairs={{4,0},{8,4},{12,8},{16,12},{20,16},{24,20},{28,24},{0,28},{5,1},{9... | collective-permute-start | bytes 3932168 | tf_op jit(solution)/shard_map/ppermute | solution.py:12
  18.8 18.2 %collective-permute-start.1 = (bf16[512,1280]{1,0:T(8,128)(2,1)}, bf16[512,1280]{1,0:T(8,128)(2,1)S(1)}, u32[]{:S(2)}, u32[]{:S(2)}) collective-permute-start(bf16[512,1280]{1,0:T(8,128)(2,1)} %collective-permute-done), channel_id=1, source_target_pairs={{4,0},{8,4},{12,8},{16,12},{20,16},{24,20},{28,24},{0,28},{5,1},{9... | collective-permute-start | bytes 3932168 | tf_op jit(solution)/shard_map/ppermute | solution.py:12
  37.1 31.0 %collective-permute-start.2 = (bf16[512,1280]{1,0:T(8,128)(2,1)S(1)}, bf16[512,1280]{1,0:T(8,128)(2,1)S(1)}, u32[]{:S(2)}, u32[]{:S(2)}) collective-permute-start(bf16[512,1280]{1,0:T(8,128)(2,1)S(1)} %collective-permute-done.1), channel_id=1, source_target_pairs={{4,0},{8,4},{12,8},{16,12},{20,16},{24,20},{28,24},{0,28},{5,1},{9... | collective-permute-start | bytes 3932168 | tf_op jit(solution)/shard_map/ppermute | solution.py:12
  39.8 2.7 %copy-start.2 = (bf16[1,512,1280]{2,1,0:T(8,128)(2,1)S(1)}, bf16[1,512,1280]{2,1,0:T(8,128)(2,1)}, u32[]{:S(2)}) copy-start(bf16[1,512,1280]{2,1,0:T(8,128)(2,1)} %param.4) | copy-start | bytes 3932164
  42.5 1.0 copy-start.1
  43.4 32.1 %collective-permute-start.3 = (bf16[1280,512]{0,1:T(8,128)(2,1)S(1)}, bf16[1280,512]{0,1:T(8,128)(2,1)S(1)}, u32[]{:S(2)}, u32[]{:S(2)}) collective-permute-start(bf16[1280,512]{0,1:T(8,128)(2,1)S(1)} %fusion.3), channel_id=1, source_target_pairs={{28,0},{0,4},{4,8},{8,12},{12,16},{16,20},{20,24},{24,28},{29,1},{... | collective-permute-start | bytes 3932168 | tf_op jit(solution)/shard_map/ppermute | solution.py:12
  45.2 50.9 %collective-permute-start.4 = (bf16[1280,512]{0,1:T(8,128)(2,1)S(1)}, bf16[1280,512]{0,1:T(8,128)(2,1)S(1)}, u32[]{:S(2)}, u32[]{:S(2)}) collective-permute-start(bf16[1280,512]{0,1:T(8,128)(2,1)S(1)} %fusion.4), channel_id=1, source_target_pairs={{24,0},{28,4},{0,8},{4,12},{8,16},{12,20},{16,24},{20,28},{25,1},{... | collective-permute-start | bytes 3932168 | tf_op jit(solution)/shard_map/ppermute | solution.py:12
  69.8 54.5 %collective-permute-start.5 = (bf16[1280,512]{0,1:T(8,128)(2,1)S(1)}, bf16[1280,512]{0,1:T(8,128)(2,1)S(1)}, u32[]{:S(2)}, u32[]{:S(2)}) collective-permute-start(bf16[1280,512]{0,1:T(8,128)(2,1)S(1)} %fusion.5), channel_id=1, source_target_pairs={{20,0},{24,4},{28,8},{0,12},{4,16},{8,20},{12,24},{16,28},{21,1},{... | collective-permute-start | bytes 3932168 | tf_op jit(solution)/shard_map/ppermute | solution.py:12
where the time goes:
time: 173 us
  waiting for transfers between devices  98.4 us (57%)
  blocking collectives  21.6 us (12%)
  local copies, waits for them, and re-layouts  16.6 us (10%)
  matrix products  12.6 us (7%)
  other arithmetic  10.2 us (6%)
  starting transfers between devices  9.87 us (6%)
  between operations  3.89 us (2%)
    ppermute x6, waiting for transfers between devices, passed_along(): return lax.ppermute(block, axis, route)  98.4 us
    all_to_all x1, blocking collectives, on_device(): lax.all_to_all(gamma, 'occ', split_axis=1, concat_axis=0, tiled=True)  21.6 us
    ppermute x6, starting transfers between devices, passed_along(): return lax.ppermute(block, axis, route)  9.87 us
    unnamed x1, other arithmetic  9.47 us
    unnamed x10, local copies, waits for them, and re-layouts  8.17 us
    dot_general x3, matrix products, on_device(): lax.dot_general(mine, partner, (((1,), (1,)), ((), ())), preferred_elemen...  4.45 us
    broadcast_in_dim x1, local copies, waits for them, and re-layouts, on_device(): gamma = (own + incoming).astype(jnp.bfloat16)[None]  4.07 us
    dot_general x3, matrix products, on_device(): lax.dot_general(partner, amps, (((0,), (1,)), ((), ())), preferred_elemen...  3.94 us
  transfers between devices with their start and end apart: 6, of which 6 were waited for; matrix products, arithmetic and copies ran while one was open for 7% of the time, Pallas kernels for 0%

commit v1 on v0

--- a/solution.py
+++ b/solution.py
@@ -1,6 +1,8 @@
 import jax
 import jax.numpy as jnp
 from jax import lax
+from jax.experimental import pallas as pl
+from jax.experimental.pallas import tpu as pltpu
 from jax.sharding import PartitionSpec as P
 
 OFFSETS = 3
@@ -50,9 +52,252 @@
     )
 
 
+LANES = 128
+ROWS = 128
+CHUNK = ROWS // 2
+
+NEAR_U = (2, 2, 3, 3, 4, 5)
+NEAR_V = (0, 1, 0, 1, 1, 0)
+SIDE_U = (2, 2, 2, 3, 3, 4)
+SIDE_V = (3, 4, 5, 4, 5, 5)
+FAR_U = (6, 6, 6, 6, 6, 7, 7, 7, 7, 7)
+FAR_V = (0, 1, 3, 4, 5, 0, 1, 2, 4, 5)
+
+
+def flipped(a, b):
+    bits = [(a // w % 2 + b // w % 2) % 2 * w for w in (1, 2, 4)]
+    return bits[0] + bits[1] + bits[2]
+
+
+def entry(table, n):
+    packed = sum(value << (3 * k) for k, value in enumerate(table))
+    return lax.shift_right_logical(jnp.int32(packed), jnp.int32(3) * n) % 8
+
+
+def gathered_kernel(
+    mine_ref, energy_ref, vir_ref, out_ref,
+    blocks, slabs, total, turned, vcol, local_sem, own_sem, fwd_sem, sib_sem, recv_sem,
+):
+    me = lax.axis_index("occ")
+    virtuals, depth = mine_ref.shape
+    width = total.shape[1]
+    window = turned.shape[0]
+    steps = virtuals // ROWS
+    chunks = virtuals // CHUNK
+    first = me * width
+    lead = pl.multiple_of(first // LANES * LANES, LANES)
+    skip = pl.multiple_of(first % LANES, 32)
+
+    barrier = pltpu.get_barrier_semaphore()
+    for bit in (1, 2, 4):
+        pl.semaphore_signal(
+            barrier, inc=1, device_id={"occ": flipped(me, bit)},
+            device_id_type=pl.DeviceIdType.MESH,
+        )
+    pl.semaphore_wait(barrier, 3)
+
+    def rows_of(q):
+        return pl.ds(pl.multiple_of(q * CHUNK, CHUNK), CHUNK)
+
+    def send(source, label, q, bit, send_sem):
+        return pltpu.make_async_remote_copy(
+            src_ref=source,
+            dst_ref=blocks.at[flipped(me, label), rows_of(q)],
+            send_sem=send_sem,
+            recv_sem=recv_sem.at[flipped(label, bit), q],
+            device_id={"occ": flipped(me, bit)},
+            device_id_type=pl.DeviceIdType.MESH,
+        )
+
+    def own_send(q, axis):
+        return send(mine_ref.at[rows_of(q)], 0, q, 2 + 2 * axis, own_sem.at[axis, q])
+
+    def far_send(q, label):
+        return send(
+            blocks.at[flipped(me, label), rows_of(q)], label, q, 6 - label, fwd_sem.at[q]
+        )
+
+    def sib_send(q, label):
+        source = mine_ref.at[rows_of(q)] if label == 0 else blocks.at[flipped(me, label), rows_of(q)]
+        return send(source, label, q, 1, sib_sem.at[label // 2, q])
+
+    def arrived(label, q):
+        place = blocks.at[flipped(me, label), rows_of(q)]
+        pltpu.make_async_copy(place, place, recv_sem.at[label, q]).wait()
+
+    @pl.loop(0, chunks)
+    def _(q):
+        own_send(q, 0).start()
+        own_send(q, 1).start()
+        sib_send(q, 0).start()
+
+    local = pltpu.make_async_copy(mine_ref, blocks.at[me], local_sem)
+    local.start()
+    total[...] = jnp.zeros_like(total)
+    for t in range(steps):
+        part = vir_ref[:, t * ROWS:(t + 1) * ROWS]
+        vcol[t * ROWS:(t + 1) * ROWS, :] = jnp.broadcast_to(part, (ROWS, ROWS)).T
+    local.wait()
+
+    def turn(label, t):
+        u = flipped(me, label)
+        rows = pl.ds(pl.multiple_of(t * ROWS, ROWS), ROWS)
+        turned[...] = blocks[u, rows, pl.ds(lead, window)].astype(jnp.float32).T
+        slabs[u, :, rows] = turned[pl.ds(skip, width), :].astype(jnp.bfloat16)
+
+    def pair(label_u, label_v, t):
+        u, v = flipped(me, label_u), flipped(me, label_v)
+        rows = pl.ds(pl.multiple_of(t * ROWS, ROWS), ROWS)
+        kmat = lax.dot_general(
+            blocks[u, rows, :], blocks[v], (((1,), (1,)), ((), ())),
+            preferred_element_type=jnp.float32,
+        )
+        denom = energy_ref[u] + energy_ref[v] - vcol[rows, 0:1] - vir_ref[...]
+        amps = (kmat / denom).astype(jnp.bfloat16)
+        total[v] += jnp.dot(slabs[u, :, rows], amps, preferred_element_type=jnp.float32)
+        total[u, :, rows] += lax.dot_general(
+            slabs[v], amps, (((1,), (1,)), ((), ())), preferred_element_type=jnp.float32
+        )
+
+    @pl.loop(0, chunks)
+    def _(q):
+        arrived(1, q)
+
+    @pl.loop(0, steps)
+    def _(t):
+        turn(0, t)
+        turn(1, t)
+
+    @pl.loop(0, steps)
+    def _(t):
+        pair(0, 1, t)
+
+    @pl.loop(0, steps)
+    def _(t):
+        for k in (0, 1):
+            q = 2 * t + k
+            arrived(2, q)
+            sib_send(q, 2).start()
+            if k == 0:
+                far_send(q, 2).start()
+            arrived(4, q)
+            sib_send(q, 4).start()
+            if k == 1:
+                far_send(q, 4).start()
+        turn(2, t)
+        turn(4, t)
+        for k in (0, 1):
+            arrived(3, 2 * t + k)
+            arrived(5, 2 * t + k)
+        turn(3, t)
+        turn(5, t)
+
+        @pl.loop(0, len(NEAR_U))
+        def _(n):
+            pair(entry(NEAR_U, n), entry(NEAR_V, n), t)
+
+    @pl.loop(0, steps)
+    def _(t):
+        @pl.loop(0, len(SIDE_U))
+        def _(n):
+            pair(entry(SIDE_U, n), entry(SIDE_V, n), t)
+
+        for k in (0, 1):
+            q = 2 * t + k
+            arrived(6, q)
+            sib_send(q, 6).start()
+        turn(6, t)
+        for k in (0, 1):
+            arrived(7, 2 * t + k)
+        turn(7, t)
+
+        @pl.loop(0, len(FAR_U))
+        def _(n):
+            pair(entry(FAR_U, n), entry(FAR_V, n), t)
+
+    @pl.loop(0, steps)
+    def _(t):
+        pair(6, 7, t)
+
+    @pl.loop(0, 2 * OFFSETS + 2)
+    def _(u):
+        out_ref[u] = total[u].astype(jnp.bfloat16)
+
+    @pl.loop(0, steps)
+    def _(t):
+        for k in (0, 1):
+            q = 2 * t + k
+            own_send(q, 0).wait_send()
+            own_send(q, 1).wait_send()
+            for label in (0, 2, 4, 6):
+                sib_send(q, label).wait_send()
+            far_send(q, 2 if k == 0 else 4).wait_send()
+
+
+def gathered(factors, occ_energy, vir_energy, coeffs):
+    _, virtuals, depth = factors.shape
+    count = lax.axis_size("occ")
+    width = depth // count
+    window = max(
+        -(-(d * width % LANES + width) // LANES) * LANES for d in range(count)
+    )
+    steps = virtuals // ROWS
+    chunks = virtuals // CHUNK
+    pair_flops = 2 * virtuals * virtuals * (depth + 2 * width)
+    gamma = pl.pallas_call(
+        gathered_kernel,
+        out_shape=jax.ShapeDtypeStruct((count, width, virtuals), jnp.bfloat16),
+        in_specs=[
+            pl.BlockSpec(memory_space=pl.ANY),
+            pl.BlockSpec(memory_space=pltpu.SMEM),
+            pl.BlockSpec(memory_space=pltpu.VMEM),
+        ],
+        out_specs=pl.BlockSpec(memory_space=pltpu.VMEM),
+        scratch_shapes=[
+            pltpu.VMEM((count, virtuals, depth), jnp.bfloat16),
+            pltpu.VMEM((count, width, virtuals), jnp.bfloat16),
+            pltpu.VMEM((count, width, virtuals), jnp.float32),
+            pltpu.VMEM((window, ROWS), jnp.float32),
+            pltpu.VMEM((virtuals, ROWS), jnp.float32),
+            pltpu.SemaphoreType.DMA,
+            pltpu.SemaphoreType.DMA((2, chunks)),
+            pltpu.SemaphoreType.DMA((chunks,)),
+            pltpu.SemaphoreType.DMA((4, chunks)),
+            pltpu.SemaphoreType.DMA((8, chunks)),
+        ],
+        compiler_params=pltpu.CompilerParams(
+            collective_id=0, has_side_effects=True, vmem_limit_bytes=44 * 1024 * 1024
+        ),
+        cost_estimate=pl.CostEstimate(
+            flops=count * OFFSETS * pair_flops, bytes_accessed=count * virtuals * depth * 2,
+            transcendentals=0,
+        ),
+    )(factors[0], occ_energy, vir_energy[None])
+    return jnp.einsum("ipa,ma->pim", gamma, coeffs, preferred_element_type=jnp.float32).astype(
+        jnp.bfloat16
+    )
+
+
+def fits(count, virtuals, depth):
+    width = depth // count
+    return (
+        count == 8
+        and count == 2 * OFFSETS + 2
+        and virtuals % ROWS == 0
+        and depth % (LANES * 2) == 0
+        and width % 32 == 0
+    )
+
+
+def either(factors, occ_energy, vir_energy, coeffs):
+    if fits(lax.axis_size("occ"), factors.shape[1], factors.shape[2]):
+        return gathered(factors, occ_energy, vir_energy, coeffs)
+    return on_device(factors, occ_energy, vir_energy, coeffs)
+
+
 def solution(mesh):
     return jax.shard_map(
-        on_device,
+        either,
         mesh=mesh,
         in_specs=(P(("frag", "occ"), None, None), P("frag"), P("frag"), P("frag", None)),
         out_specs=P("occ", "frag", None),

time: 173 us -> 110 us (0.64)
  Pallas kernels: 0 us -> 103 us
  waiting for transfers between devices: 98.4 us -> 0 us
  blocking collectives: 21.6 us -> 0 us
  matrix products: 12.6 us -> 1.56 us
  local copies, waits for them, and re-layouts: 16.6 us -> 5.67 us
  other arithmetic: 10.2 us -> 0 us
  starting transfers between devices: 9.87 us -> 0 us
  between operations: 3.89 us -> 0.03 us
    pallas_call x0 -> x1, Pallas kernels: none -> 103 us  [gathered(): pl.pallas_call(gathered_kernel, out_shape=jax.ShapeDtypeStruct((count, wi...]
    ppermute x6 -> x0, waiting for transfers between devices: 98.4 us -> none  [passed_along(): return lax.ppermute(block, axis, route)]
    all_to_all x1 -> x0, blocking collectives: 21.6 us -> none  [on_device(): lax.all_to_all(gamma, 'occ', split_axis=1, concat_axis=0, tiled=True)]
    dot_general x10 -> x1, matrix products: 12.6 us -> 1.56 us  [gathered(): jnp.einsum('ipa,ma->pim', gamma, coeffs, preferred_element_type=jnp.float32)]
    ppermute x6 -> x0, starting transfers between devices: 9.87 us -> none  [passed_along(): return lax.ppermute(block, axis, route)]
    unnamed x1 -> x0, other arithmetic: 9.47 us -> none
    unnamed x10 -> x8, local copies, waits for them, and re-layouts: 8.17 us -> 2.74 us
    broadcast_in_dim x1 -> x0, local copies, waits for them, and re-layouts: 4.07 us -> none  [on_device(): gamma = (own + incoming).astype(jnp.bfloat16)[None]]
  transfers between devices with their start and end apart: 6 -> 0, of which waited for: 6 -> 0; matrix products, arithmetic and copies ran while one was open for 7% -> 0% of each run, Pallas kernels for 0% -> 0%
where the time goes in v1:
time: 110 us
  Pallas kernels  103 us (94%)
  local copies, waits for them, and re-layouts  5.67 us (5%)
  matrix products  1.56 us (1%)
    pallas_call x1, Pallas kernels, gathered(): pl.pallas_call(gathered_kernel, out_shape=jax.ShapeDtypeStruct((count, wi...  103 us
    convert_element_type x1, local copies, waits for them, and re-layouts, gathered(): jnp.einsum('ipa,ma->pim', gamma, coeffs, preferred_element_type=jnp.float32)  2.93 us
    unnamed x8, local copies, waits for them, and re-layouts  2.74 us

profile of v1, /device:TPU:0, one launch (start us, length us, event | category | flops | bytes accessed | tf_op | source)
XLA Modules:
  0.0 110.2 jit_solution(7043819989291811862)
XLA Ops:
  0.0 0.0 copy-start
  0.0 0.0 copy-start.1
  0.0 1.4 %copy-done.1 = bf16[1,512,1280]{2,1,0:T(8,128)(2,1)S(1)} copy-done((bf16[1,512,1280]{2,1,0:T(8,128)(2,1)S(1)}, bf16[1,512,1280]{2,1,0:T(8,128)(2,1)}, u32[]{:S(2)}) %copy-start.1) | copy-done | bytes 1310744
  1.4 0.0 copy-start.2
  1.4 0.7 copy-done.2
  2.1 0.0 copy-start.3
  2.1 0.7 copy-done.3
  2.7 102.9 %shard_map.46 = bf16[8,160,512]{2,1,0:T(8,128)(2,1)S(1)} custom-call(bf16[512,1280]{1,0:T(8,128)(2,1)S(1)} %bitcast.8, f32[8]{0:T(128)S(1)} %copy-done.3, f32[1,512]{1,0:T(1,128)S(1)} %bitcast.9), custom_call_target="tpu_custom_call" | custom-call | flops 20132659200 | bytes 10485760 | tf_op jit(solution)/shard_map/pallas_call | solution.py:247
  105.7 0.0 copy-done
  105.7 1.6 %convert_bitcast_fusion = bf16[160,8,1024]{2,0,1:T(8,128)(2,1)S(1)} fusion(bf16[8,160,512]{2,1,0:T(8,128)(2,1)S(1)} %shard_map.46, bf16[1024,512]{1,0:T(8,128)(2,1)S(1)} %copy-done), kind=kOutput, calls=%fused_computation | convolution fusion | flops 1343488000 | bytes 4980736 | tf_op jit(solution)/shard_map/ipa,ma->pim/dot_general | solution.py:276
  107.3 2.9 %copy.5 = bf16[160,8,1024]{2,1,0:T(8,128)(2,1)} copy(bf16[160,8,1024]{2,0,1:T(8,128)(2,1)S(1)} %convert_bitcast_fusion) | data formatting | bytes 5242880 | tf_op jit(solution)/shard_map/convert_element_type | solution.py:276
Async XLA Ops:
  0.0 105.7 %copy-start = (bf16[1024,512]{1,0:T(8,128)(2,1)S(1)}, bf16[1024,512]{1,0:T(8,128)(2,1)}, u32[]{:S(2)}) copy-start(bf16[1024,512]{1,0:T(8,128)(2,1)} %param.7) | copy-start | bytes 3145732
  0.0 1.4 %copy-start.1 = (bf16[1,512,1280]{2,1,0:T(8,128)(2,1)S(1)}, bf16[1,512,1280]{2,1,0:T(8,128)(2,1)}, u32[]{:S(2)}) copy-start(bf16[1,512,1280]{2,1,0:T(8,128)(2,1)} %param.4) | copy-start | bytes 3932164
  1.4 0.7 copy-start.2
  2.1 0.7 copy-start.3
